TPU v7x, 32 devices: a whole 2x2x4 slice. The times are simulated.
32 devices in a mesh: grp: 1, sp: 32 (over z, y, x, core), ch: 1.
Axes of the slice: x: 2, y: 2, z: 4, core: 2. Of those that a mesh axis runs over, the one named last changes fastest.
Arguments:
- latents: bfloat16 [131072, 1024], P(('grp', 'sp')), may hold values from -6 to 6
- spectrum: bfloat16 [16, 64, 128, 1024], P(None, None, 'sp', 'ch'), may hold values from -4 to 4
- w_value: bfloat16 [1024, 1024], P('sp', 'ch'), may hold values from -0.1875 to 0.1875
- w_gate: bfloat16 [1024, 1024], P('sp', 'ch'), may hold values from -0.1875 to 0.1875
- w_out: bfloat16 [1024, 1024], P('sp'), may hold values from -0.1875 to 0.1875
- embed_table: bfloat16 [1024, 32768], P(('sp', 'ch')), may hold values from -12 to 12
- prompt_ids: int32 [256], P('grp'), may hold values from 0 to 32767
- noise_step: int32 [1], P('grp'), may hold values from 0 to 999
Outputs:
- denoised: bfloat16 [131072, 1024], P(('grp', 'sp', 'ch'))
All inputs are finite; a program needn't handle non-finite values.
Results may differ from a plain program's by a relative error of at most 0.013.
Values may be sent and summed in bfloat16 or wider, within the bound.
A program may use at most 128 MiB of HBM per device.

v0:
```python
import math

import jax
import jax.numpy as jnp
from jax import lax
from jax.experimental import pallas as pl
from jax.experimental.pallas import tpu as pltpu
from jax.sharding import PartitionSpec as P

TT = 16
HH = 64
WW = 128
C = 1024

TILE = 16


def cas_table(length):
    position = jnp.arange(length, dtype=jnp.int32)
    product = position[:, None] * position[None, :] % length
    phase_angle = product.astype(jnp.float32) * (2.0 * math.pi / length)
    return ((jnp.cos(phase_angle) + jnp.sin(phase_angle)) / math.sqrt(length)).astype(jnp.bfloat16)


def step_embedding(noise_step, channel, channels):
    half_count = channels // 2
    lower_half = channel < half_count
    position = jnp.where(lower_half, channel, channel - half_count).astype(jnp.float32)
    frequency = jnp.exp(-math.log(10000.0) * position / half_count)
    phase_angle = noise_step[0].astype(jnp.float32) * frequency
    return jnp.where(lower_half, jnp.sin(phase_angle), jnp.cos(phase_angle))


def widened(table, copies):
    length = table.shape[0]
    inner = jnp.eye(copies, dtype=table.dtype)
    both = table[:, None, :, None] * inner[None, :, None, :]
    return both.reshape(length * copies, length * copies)


def dot(left, right):
    return jnp.dot(left, right, preferred_element_type=jnp.float32)


def width_kernel(table_ref, latents_ref, out_ref):
    owners, rows, channels = out_ref.shape
    moved = dot(table_ref[...], latents_ref[...])
    out_ref[...] = moved.reshape(owners, rows, channels).astype(out_ref.dtype)


def width_forward(table, latents, owners, lines, band, group):
    channels = latents.shape[1]
    rows = group * WW
    cells = lines * WW
    return pl.pallas_call(
        width_kernel,
        grid=(lines // group,),
        in_specs=[
            pl.BlockSpec(table.shape, lambda g: (0, 0)),
            pl.BlockSpec((rows, channels), lambda g: (g, 0)),
        ],
        out_specs=pl.BlockSpec((owners, group * band, channels), lambda g: (0, g, 0)),
        out_shape=jax.ShapeDtypeStruct((owners, lines * band, channels), jnp.bfloat16),
        compiler_params=pltpu.CompilerParams(vmem_limit_bytes=48 * 2**20),
        cost_estimate=pl.CostEstimate(
            flops=2 * cells * table.shape[0] * channels,
            bytes_accessed=4 * cells * channels,
            transcendentals=0,
        ),
        name="width_forward",
    )(table, latents)


def plane_kernel(band, height_ref, time_ref, planes_ref, weight_ref, spectrum_ref, out_ref, spec):
    per_frame = HH * band
    width = out_ref.shape[1]
    pieces = per_frame // TILE
    weight = weight_ref[...].reshape(planes_ref.shape[1], width)

    def forward(t, carry):
        rows = pl.ds(pl.multiple_of(t * per_frame, per_frame), per_frame)
        value = dot(planes_ref[rows, :], weight).astype(jnp.bfloat16)
        spec[t] = dot(height_ref[...], value).astype(jnp.bfloat16)
        return carry

    lax.fori_loop(0, TT, forward, 0, unroll=4)

    def across(p, carry):
        rows = pl.ds(pl.multiple_of(p * TILE, TILE), TILE)
        block = spec[:, rows, :].reshape(TT * TILE, width)
        full = dot(time_ref[...], block)
        gain = spectrum_ref[:, rows, :].reshape(TT * TILE, width).astype(jnp.float32)
        filtered = (full * gain).astype(jnp.bfloat16)
        back = dot(time_ref[...], filtered).astype(jnp.bfloat16)
        spec[:, rows, :] = back.reshape(TT, TILE, width)
        return carry

    lax.fori_loop(0, pieces, across, 0, unroll=4)

    def backward(t, carry):
        rows = pl.ds(pl.multiple_of(t * per_frame, per_frame), per_frame)
        out_ref[rows, :] = dot(height_ref[...], spec[t]).astype(jnp.bfloat16)
        return carry

    lax.fori_loop(0, TT, backward, 0, unroll=4)


def plane_filter(height, time, planes, weight, spectrum, band):
    cells, channels = planes.shape
    shards, depth, chan_part = weight.shape
    width = min(256, chan_part)
    per_frame = HH * band
    return pl.pallas_call(
        lambda *refs: plane_kernel(band, *refs),
        grid=(chan_part // width,),
        in_specs=[
            pl.BlockSpec(height.shape, lambda g: (0, 0)),
            pl.BlockSpec(time.shape, lambda g: (0, 0)),
            pl.BlockSpec((cells, channels), lambda g: (0, 0)),
            pl.BlockSpec((shards, depth, width), lambda g: (0, 0, g)),
            pl.BlockSpec((TT, per_frame, width), lambda g: (0, 0, g)),
        ],
        out_specs=pl.BlockSpec((cells, width), lambda g: (0, g)),
        out_shape=jax.ShapeDtypeStruct((cells, chan_part), jnp.bfloat16),
        scratch_shapes=[pltpu.VMEM((TT, per_frame, width), jnp.bfloat16)],
        cost_estimate=pl.CostEstimate(
            flops=2 * cells * chan_part * (channels + 1024),
            bytes_accessed=2 * cells * (channels + 2 * chan_part),
            transcendentals=0,
        ),
        compiler_params=pltpu.CompilerParams(vmem_limit_bytes=56 * 2**20),
        name="plane_filter",
    )(height, time, planes, weight, spectrum)


def gate_kernel(latents_ref, gate_ref, scale_ref, out_ref):
    gate = dot(latents_ref[...], gate_ref[...].reshape(latents_ref.shape[1], out_ref.shape[1]))
    gate = gate / (1.0 + jnp.exp(-gate))
    out_ref[...] = (gate * scale_ref[...]).astype(out_ref.dtype)


def gate_rows(latents, gate_w, scale):
    cells, channels = latents.shape
    chan_part = gate_w.shape[2]
    rows = min(512, cells)
    return pl.pallas_call(
        gate_kernel,
        grid=(cells // rows,),
        in_specs=[
            pl.BlockSpec((rows, channels), lambda g: (g, 0)),
            pl.BlockSpec(gate_w.shape, lambda g: (0, 0, 0)),
            pl.BlockSpec((1, chan_part), lambda g: (0, 0)),
        ],
        out_specs=pl.BlockSpec((rows, chan_part), lambda g: (g, 0)),
        out_shape=jax.ShapeDtypeStruct((cells, chan_part), jnp.bfloat16),
        compiler_params=pltpu.CompilerParams(vmem_limit_bytes=48 * 2**20),
        cost_estimate=pl.CostEstimate(
            flops=2 * cells * channels * chan_part,
            bytes_accessed=2 * cells * (channels + chan_part),
            transcendentals=cells * chan_part,
        ),
        name="gate_rows",
    )(latents, gate_w, scale)


def mix_kernel(parts, residual, *refs):
    tables, backs = refs[:parts], refs[parts : 2 * parts]
    latents_ref, gate_ref, out_w_ref, out_ref = refs[2 * parts :]
    owners, rows, chan_part = backs[0].shape
    mix = dot(tables[0][...], backs[0][...].reshape(owners * rows, chan_part))
    for table_ref, back_ref in zip(tables[1:], backs[1:]):
        mix += dot(table_ref[...], back_ref[...].reshape(owners * rows, chan_part))
    mixed = (mix * gate_ref[...].astype(jnp.float32)).astype(jnp.bfloat16)
    projected = dot(mixed, out_w_ref[...].reshape(chan_part, out_ref.shape[1]))
    if residual:
        projected = latents_ref[...].astype(jnp.float32) + projected
    out_ref[...] = projected.astype(out_ref.dtype)


def mix_and_project(tables, backs, latents, gate, out_w, out_depth, group, residual):
    parts = len(backs)
    owners, rows_all, chan_part = backs[0].shape
    cells, channels = latents.shape
    groups = cells // (group * WW)
    rows = rows_all // groups
    cell_block = lambda wide: pl.BlockSpec((group * WW, wide), lambda g: (g, 0))
    return pl.pallas_call(
        lambda *refs: mix_kernel(parts, residual, *refs),
        grid=(groups,),
        in_specs=[
            *[pl.BlockSpec(table.shape, lambda g: (0, 0)) for table in tables],
            *[pl.BlockSpec((owners, rows, chan_part), lambda g: (0, g, 0)) for _ in backs],
            cell_block(channels),
            cell_block(chan_part),
            pl.BlockSpec((out_w.shape[0], out_depth, channels), lambda g: (0, 0, 0)),
        ],
        out_specs=cell_block(channels),
        out_shape=jax.ShapeDtypeStruct((cells, channels), jnp.bfloat16),
        compiler_params=pltpu.CompilerParams(vmem_limit_bytes=56 * 2**20),
        name="mix_and_project",
    )(*tables, *backs, latents, gate, out_w)


def exchange(blocks):
    return lax.all_to_all(blocks, "sp", split_axis=0, concat_axis=0, tiled=True)


def local(latents, spectrum, w_value, w_gate, w_out, embed_table, prompt_ids, noise_step):
    row_count, channels = latents.shape
    chan_part = w_value.shape[1]
    owners = lax.axis_size("sp")
    splits = lax.axis_size("ch")
    lines = row_count // WW
    band = WW // owners
    group = min(lines, max(1, TILE // band))

    parts = 2 if band % 2 == 0 else 1
    sub = band // parts

    table = cas_table(WW).reshape(owners, parts, 1, sub, 1, WW)
    same_line = jnp.eye(group, dtype=jnp.bfloat16).reshape(1, group, 1, group, 1)
    width_tables = [
        (table[:, part] * same_line).reshape(owners * group * sub, group * WW)
        for part in range(parts)
    ]
    height_table = widened(cas_table(HH), sub)
    time_table = widened(cas_table(TT), TILE)
    gains = spectrum.reshape(TT, HH, parts, sub, chan_part)

    full_value = lax.all_gather(w_value, "sp", axis=0)

    full_gate = lax.all_gather(w_gate, "sp", axis=0)
    local_pool = jnp.mean(jnp.take(embed_table, prompt_ids, axis=1).astype(jnp.float32), axis=1)
    offset = lax.axis_index("ch") * chan_part
    depth = w_out.shape[0]
    if splits == 1:
        first = local_pool.astype(jnp.bfloat16)
        rest = local_pool - first.astype(jnp.float32)
        second = rest.astype(jnp.bfloat16)
        third = (rest - second.astype(jnp.float32)).astype(jnp.bfloat16)
        terms = jnp.stack([first, second, third])
        terms = jnp.pad(terms, ((0, TILE - 3), (0, channels - terms.shape[1])))
        full_out = lax.all_gather(jnp.concatenate([w_out, terms], axis=0), "sp", axis=0)
    else:
        pooled_all = lax.all_gather(local_pool, ("sp", "ch"), axis=0, tiled=True)
        pooled = lax.dynamic_slice_in_dim(pooled_all, offset, chan_part)
        rows_out = lax.all_gather(w_out, "sp", axis=0, tiled=True)
        full_out = lax.dynamic_slice_in_dim(rows_out, offset, chan_part, 0)[None]
        depth = chan_part

    planes, backs = [], []
    for part in range(parts):
        sent = width_forward(width_tables[part], latents, owners, lines, sub, group)
        if planes:
            sent, planes[-1], full_value = lax.optimization_barrier((sent, planes[-1], full_value))
        planes.append(exchange(sent))
    for part in range(parts):
        filtered = plane_filter(
            height_table,
            time_table,
            planes[part].reshape(TT * HH * sub, channels),
            full_value,
            gains[:, :, part].reshape(TT, HH * sub, chan_part),
            sub,
        ).reshape(owners, lines * sub, chan_part)
        if backs:
            filtered, backs[-1], full_gate = lax.optimization_barrier(
                (filtered, backs[-1], full_gate)
            )
        elif parts > 1:
            filtered, planes[-1], full_out = lax.optimization_barrier(
                (filtered, planes[-1], full_out)
            )
        backs.append(exchange(filtered))

    if splits == 1:
        pooled = full_out[:, depth : depth + 3, : local_pool.shape[0]].astype(jnp.float32)
        pooled = jnp.sum(pooled, axis=1).reshape(chan_part)
    channel = offset + jnp.arange(chan_part, dtype=jnp.int32)
    modulation = 1.0 + pooled + step_embedding(noise_step, channel, C)

    gate = gate_rows(latents, full_gate, modulation[None, :])
    mixed = mix_and_project(
        [width_table.T for width_table in width_tables],
        backs,
        latents,
        gate,
        full_out,
        depth,
        group,
        splits == 1,
    )
    if splits == 1:
        return mixed
    half_rows = row_count // splits
    summed = lax.psum_scatter(mixed, "ch", scatter_dimension=0, tiled=True).astype(jnp.float32)
    residual = lax.dynamic_slice_in_dim(latents, lax.axis_index("ch") * half_rows, half_rows, 0)
    return (residual.astype(jnp.float32) + summed).astype(jnp.bfloat16)


def solution(mesh):
    placed = (
        P(("grp", "sp"), None),
        P(None, None, "sp", "ch"),
        P("sp", "ch"),
        P("sp", "ch"),
        P("sp", None),
        P(("sp", "ch"), None),
        P("grp"),
        P("grp"),
    )
    return jax.shard_map(
        local, mesh=mesh, in_specs=placed, out_specs=P(("grp", "sp", "ch"), None), check_vma=False
    )
```

profile of v0, /device:TPU:0, one launch (start us, length us, event | category | flops | bytes accessed | tf_op | source)
XLA Modules:
  0.0 472.2 jit_solution(7177597898888992940)
XLA Ops:
  6.5 0.3 multiply_convert_fusion
  7.0 0.3 broadcast_multiply_fusion.2
  7.3 7.5 %width_forward.3 = bf16[32,64,1024]{2,1,0:T(8,128)(2,1)S(1)} custom-call(bf16[256,512]{1,0:T(8,128)(2,1)S(1)} %bitcast.45, bf16[4096,1024]{1,0:T(8,128)(2,1)} %refs_4_.1), custom_call_target="tpu_custom_call" | custom-call | flops 2147483648 | bytes 16777216 | tf_op jit(solution)/shard_map/width_forward/pallas_call | solution.py:55
  14.8 0.0 copy-start.1
  14.8 2.0 copy-done.1
  16.8 7.5 %all-to-all-start = ((bf16[32,64,1024]{2,1,0:T(8,128)(2,1)}), bf16[32,64,1024]{2,1,0:T(8,128)(2,1)}, u32[]{:S(2)}, u32[]{:S(2)}) async-start(bf16[32,64,1024]{2,1,0:T(8,128)(2,1)} %copy-done.1), calls=%async_computation | async-start | bytes 8388608 | tf_op jit(solution)/shard_map/all_to_all | solution.py:205
  24.2 0.0 all-gather.7.cloned.1.call-start
  24.3 0.7 all-gather.7.cloned.1.call-update
  25.0 7.5 %width_forward.2 = bf16[32,64,1024]{2,1,0:T(8,128)(2,1)S(1)} custom-call(bf16[256,512]{1,0:T(8,128)(2,1)S(1)} %bitcast.47, bf16[4096,1024]{1,0:T(8,128)(2,1)} %refs_4_.1), custom_call_target="tpu_custom_call" | custom-call | flops 2147483648 | bytes 16777216 | tf_op jit(solution)/shard_map/width_forward/pallas_call | solution.py:55
  32.5 0.0 copy-start
  32.5 2.0 copy-done
  34.5 78.1 %all-gather.7.cloned.1.call-done = bf16[1024,1024]{1,0:T(8,128)(2,1)} async-done(((bf16[32,1024]{1,0:T(8,128)(2,1)}), bf16[1024,1024]{1,0:T(8,128)(2,1)}) %all-gather.7.cloned.1.call-update) | async-done | bytes 2097168 | tf_op jit(solution)/shard_map/all_gather | solution.py:230
  112.6 15.4 %all-to-all-done = bf16[32,64,1024]{2,1,0:T(8,128)(2,1)} async-done(((bf16[32,64,1024]{2,1,0:T(8,128)(2,1)}), bf16[32,64,1024]{2,1,0:T(8,128)(2,1)}, u32[]{:S(2)}, u32[]{:S(2)}) %all-to-all-start) | async-done | bytes 4194336 | tf_op jit(solution)/shard_map/all_to_all | solution.py:205
  128.0 0.0 copy-start.3
  128.0 3.9 all-to-all-start.1
  131.9 0.0 copy-start.5
  131.9 0.0 copy-start.4
  131.9 0.0 all-gather.9.cloned.1.call-start
  131.9 0.0 copy-done.3
  132.0 5.9 %copy.24 = bf16[32,32768]{0,1:T(8,128)(2,1)} copy(bf16[32,32768]{1,0:T(8,128)(2,1)S(1)} %copy-done.3) | data formatting | bytes 4194304 | tf_op args[5]
  137.9 0.0 copy-done.5
  137.9 5.2 %gather_fusion = bf16[256,32]{1,0:T(8,128)(2,1)S(1)} fusion(bf16[32,32768]{0,1:T(8,128)(2,1)} %copy.24, s32[1024]{0:T(1024)S(1)} %pad_clamp_fusion), kind=kCustom, calls=%fused_computation | custom fusion | bytes 33792 | tf_op jit(solution)/shard_map/jit(_take)/gather | solution.py:233
  143.1 0.1 convert_reduce_fusion
  143.2 0.0 copy-done.4
  143.3 0.6 pad_maximum_fusion
  143.9 0.0 all-gather.9.cloned.1.call-update
  143.9 17.5 %reshape.298 = bf16[16,64,2,2,1024]{4,3,2,1,0:T(2,128)(2,1)} reshape(bf16[16,64,4,1024]{3,2,1,0:T(4,128)(2,1)} %param.9) | data formatting | bytes 16777216 | tf_op jit(solution)/shard_map/reshape | solution.py:228
  161.4 8.4 %slice_bitcast_fusion = (bf16[16,64,1,2,1024]{4,3,1,0,2:T(2,128)(2,1)}, bf16[16,64,1,2,1024]{4,3,1,0,2:T(2,128)(2,1)}) fusion(bf16[16,64,2,2,1024]{4,3,2,1,0:T(2,128)(2,1)} %reshape.298), kind=kLoop, calls=%fused_computation.1 | loop fusion | bytes 16777216
  169.8 7.2 %reshape_squeeze.6.refs_4_ = bf16[16,128,1024]{2,1,0:T(8,128)(2,1)} reshape(bf16[16,64,1,2,1024]{4,3,1,0,2:T(2,128)(2,1)} %get-tuple-element.24) | data formatting | bytes 8388608 | tf_op jit(solution)/shard_map/reshape;squeeze | solution.py:263
  177.0 0.2 multiply_convert_fusion.1
  177.2 0.7 broadcast_multiply_fusion
  177.9 3.8 mul.316.refs_0_
  181.7 0.1 multiply_convert_fusion.2
  181.7 0.1 broadcast_multiply_fusion.1
  181.9 1.6 mul.325.refs_1_
  183.5 38.9 %plane_filter.2 = bf16[2048,1024]{1,0:T(8,128)(2,1)} custom-call(bf16[128,128]{1,0:T(8,128)(2,1)} %mul.316.refs_0_, bf16[256,256]{1,0:T(8,128)(2,1)} %mul.325.refs_1_, bf16[2048,1024]{1,0:T(8,128)(2,1)} %bitcast.5.refs_2_, bf16[32,32,1024]{2,1,0:T(8,128)(2,1)} %bitcast.58, bf16[16,128,1024]{2,1,0:T(8,128)(2,1)} %reshape_squeeze.6.refs_4_), custom_call_target="tpu_custom_call" | custom-call | flops 8589934592 | bytes 12582912 | tf_op jit(solution)/shard_map/plane_filter/pallas_call | solution.py:113
  222.4 2.4 all-gather.9.cloned.1.call-done
  224.8 15.5 %all-to-all-done.1 = bf16[32,64,1024]{2,1,0:T(8,128)(2,1)} async-done(((bf16[32,64,1024]{2,1,0:T(8,128)(2,1)}), bf16[32,64,1024]{2,1,0:T(8,128)(2,1)}, u32[]{:S(2)}, u32[]{:S(2)}) %all-to-all-start.1) | async-done | bytes 4194336 | tf_op jit(solution)/shard_map/all_to_all | solution.py:205
  240.3 4.3 all-to-all-start.2
  244.6 0.2 all-gather.11.cloned.1.call-start
  244.8 0.5 all-gather.11.cloned.1.call-update
  245.3 7.2 %reshape_squeeze.7.refs_4_ = bf16[16,128,1024]{2,1,0:T(8,128)(2,1)} reshape(bf16[16,64,1,2,1024]{4,3,1,0,2:T(2,128)(2,1)} %get-tuple-element.23) | data formatting | bytes 8388608 | tf_op jit(solution)/shard_map/reshape;squeeze | solution.py:263
  252.5 39.0 %plane_filter.3 = bf16[2048,1024]{1,0:T(8,128)(2,1)} custom-call(bf16[128,128]{1,0:T(8,128)(2,1)} %mul.316.refs_0_, bf16[256,256]{1,0:T(8,128)(2,1)} %mul.325.refs_1_, bf16[2048,1024]{1,0:T(8,128)(2,1)} %bitcast.9.refs_2_, bf16[32,32,1024]{2,1,0:T(8,128)(2,1)} %bitcast.59, bf16[16,128,1024]{2,1,0:T(8,128)(2,1)} %reshape_squeeze.7.refs_4_), custom_call_target="tpu_custom_call" | custom-call | flops 8589934592 | bytes 12582912 | tf_op jit(solution)/shard_map/plane_filter/pallas_call | solution.py:113
  291.5 41.5 %all-gather.11.cloned.1.call-done = bf16[1024,1024]{1,0:T(8,128)(2,1)} async-done(((bf16[32,1024]{1,0:T(8,128)(2,1)}), bf16[1024,1024]{1,0:T(8,128)(2,1)}) %all-gather.11.cloned.1.call-update) | async-done | bytes 2097168 | tf_op jit(solution)/shard_map/all_gather | solution.py:232
  333.0 15.4 %all-to-all-done.2.refs_2_ = bf16[32,64,1024]{2,1,0:T(8,128)(2,1)} async-done(((bf16[32,64,1024]{2,1,0:T(8,128)(2,1)}), bf16[32,64,1024]{2,1,0:T(8,128)(2,1)}, u32[]{:S(2)}, u32[]{:S(2)}) %all-to-all-start.2) | async-done | bytes 4194336 | tf_op jit(solution)/shard_map/all_to_all | solution.py:205
  348.3 0.0 copy-start.2
  348.3 3.9 all-to-all-start.3
  352.2 0.8 copy.20
  353.0 0.8 copy.22
  354.5 0.9 convert_reduce_fusion.1
  355.4 0.1 add.143
  355.5 0.1 fusion.32.scale_ref
  355.6 0.0 copy-done.2
  355.7 14.7 %gate_rows.1.refs_5_ = bf16[4096,1024]{1,0:T(8,128)(2,1)} custom-call(bf16[4096,1024]{1,0:T(8,128)(2,1)} %refs_4_.1, bf16[32,32,1024]{2,1,0:T(8,128)(2,1)S(1)} %bitcast.49, f32[1,1024]{1,0:T(1,128)S(1)} %fusion.32.scale_ref), custom_call_target="tpu_custom_call" | custom-call | flops 8589934592 | bytes 16777216 | tf_op jit(solution)/shard_map/gate_rows/pallas_call | solution.py:146
  370.4 75.5 %all-to-all-done.3.refs_3_ = bf16[32,64,1024]{2,1,0:T(8,128)(2,1)} async-done(((bf16[32,64,1024]{2,1,0:T(8,128)(2,1)}), bf16[32,64,1024]{2,1,0:T(8,128)(2,1)}, u32[]{:S(2)}, u32[]{:S(2)}) %all-to-all-start.3) | async-done | bytes 4194336 | tf_op jit(solution)/shard_map/all_to_all | solution.py:205
  445.9 19.8 %mix_and_project.1 = bf16[4096,1024]{1,0:T(8,128)(2,1)} custom-call(bf16[512,256]{1,0:T(8,128)(2,1)} %bitcast.54, bf16[512,256]{1,0:T(8,128)(2,1)} %bitcast.55, bf16[32,64,1024]{2,1,0:T(8,128)(2,1)} %all-to-all-done.2.refs_2_, bf16[32,64,1024]{2,1,0:T(8,128)(2,1)} %all-to-all-done.3.refs_3_, bf16[4096,1024]{1,0:T(8,128)(2,1)} %refs_4_.1, ...), custom_call_target="tpu_custom_call" | custom-call | tf_op jit(solution)/shard_map/mix_and_project/pallas_call | solution.py:187
  (16 shorter events, 0.2 us)
Async XLA Ops:
  14.8 2.0 copy-start.1
  16.8 111.2 %all-to-all-start = ((bf16[32,64,1024]{2,1,0:T(8,128)(2,1)}), bf16[32,64,1024]{2,1,0:T(8,128)(2,1)}, u32[]{:S(2)}, u32[]{:S(2)}) async-start(bf16[32,64,1024]{2,1,0:T(8,128)(2,1)} %copy-done.1), calls=%async_computation | async-start | bytes 8388608 | tf_op jit(solution)/shard_map/all_to_all | solution.py:205
  24.2 88.4 %all-gather.7.cloned.1.call-start = ((), (), s32[]{:S(2)}) async-start(), calls=%async_computation.4 | async-start | bytes 2162688 | tf_op jit(solution)/shard_map/all_gather | solution.py:230
  32.5 2.0 copy-start
  128.0 4.0 copy-start.3
  128.0 112.3 %all-to-all-start.1 = ((bf16[32,64,1024]{2,1,0:T(8,128)(2,1)}), bf16[32,64,1024]{2,1,0:T(8,128)(2,1)}, u32[]{:S(2)}, u32[]{:S(2)}) async-start(bf16[32,64,1024]{2,1,0:T(8,128)(2,1)} %copy-done), calls=%async_computation.1 | async-start | bytes 8388608 | tf_op jit(solution)/shard_map/all_to_all | solution.py:205
  131.9 6.0 %copy-start.5 = (s32[256]{0:T(256)S(1)}, s32[256]{0:T(256)}, u32[]{:S(2)}) copy-start(s32[256]{0:T(256)} %param.14) | copy-start | bytes 3076
  131.9 11.4 %copy-start.4 = (bf16[32,1024]{1,0:T(8,128)(2,1)S(1)}, bf16[32,1024]{1,0:T(8,128)(2,1)}, u32[]{:S(2)}) copy-start(bf16[32,1024]{1,0:T(8,128)(2,1)} %param.12) | copy-start | bytes 196612
  131.9 92.9 %all-gather.9.cloned.1.call-start = ((), (), s32[]{:S(2)}) async-start(), calls=%async_computation.5 | async-start | bytes 3244032 | tf_op jit(solution)/shard_map/all_gather | solution.py:243
  240.3 108.0 %all-to-all-start.2 = ((bf16[32,64,1024]{2,1,0:T(8,128)(2,1)}), bf16[32,64,1024]{2,1,0:T(8,128)(2,1)}, u32[]{:S(2)}, u32[]{:S(2)}) async-start(bf16[32,64,1024]{2,1,0:T(8,128)(2,1)} %bitcast.50), calls=%async_computation.2 | async-start | bytes 8388608 | tf_op jit(solution)/shard_map/all_to_all | solution.py:205
  244.6 88.4 %all-gather.11.cloned.1.call-start = ((), (), s32[]{:S(2)}) async-start(), calls=%async_computation.6 | async-start | bytes 2162688 | tf_op jit(solution)/shard_map/all_gather | solution.py:232
  348.3 7.3 %copy-start.2 = (bf16[1024,1024]{1,0:T(8,128)(2,1)S(1)}, bf16[1024,1024]{1,0:T(8,128)(2,1)}, u32[]{:S(2)}) copy-start(bf16[1024,1024]{1,0:T(8,128)(2,1)} %all-gather.11.cloned.1.call-done) | copy-start | bytes 6291460
  348.3 97.6 %all-to-all-start.3 = ((bf16[32,64,1024]{2,1,0:T(8,128)(2,1)}), bf16[32,64,1024]{2,1,0:T(8,128)(2,1)}, u32[]{:S(2)}, u32[]{:S(2)}) async-start(bf16[32,64,1024]{2,1,0:T(8,128)(2,1)} %bitcast.51), calls=%async_computation.3 | async-start | bytes 8388608 | tf_op jit(solution)/shard_map/all_to_all | solution.py:205
Sparse Core Ops, SparseCore 0:
  27.9 84.6 all-gather.6
  144.1 80.7 all-gather.8
  248.2 84.6 all-gather.10
where the time goes:
time: 474 us; the launch traced here: 472 us
  waiting for transfers between devices  245 us (52%)
  Pallas kernels  127 us (27%)
  local copies, waits for them, and re-layouts  62.6 us (13%)
  starting transfers between devices  19.8 us (4%)
  between operations  14 us (3%)
    all_to_all x4, waiting for transfers between devices, exchange(): return lax.all_to_all(blocks, 'sp', split_axis=0, concat_axis=0, tiled=True)  122 us
    all_gather x1, waiting for transfers between devices, local(): full_value = lax.all_gather(w_value, 'sp', axis=0)  78.1 us
    pallas_call x2, Pallas kernels, plane_filter(): pl.pallas_call(lambda *refs: plane_kernel(band, *refs), grid=(chan_part /...  77.9 us
    all_gather x1, waiting for transfers between devices, local(): full_gate = lax.all_gather(w_gate, 'sp', axis=0)  41.5 us
    pallas_call x1, Pallas kernels, mix_and_project(): pl.pallas_call(lambda *refs: mix_kernel(parts, residual, *refs), grid=(gr...  19.8 us
    all_to_all x4, starting transfers between devices, exchange(): return lax.all_to_all(blocks, 'sp', split_axis=0, concat_axis=0, tiled=True)  19.5 us
    unnamed x16, local copies, waits for them, and re-layouts  18.4 us
    reshape x1, local copies, waits for them, and re-layouts, local(): gains = spectrum.reshape(TT, HH, parts, sub, chan_part)  17.5 us
  transfers between devices with their start and end apart: 7, of which 7 were waited for; matrix products, arithmetic and copies ran while one was open for 13% of the time, Pallas kernels for 21%

commit v1 on v0

--- a/solution.py
+++ b/solution.py
@@ -2,6 +2,7 @@
 
 import jax
 import jax.numpy as jnp
+import numpy as np
 from jax import lax
 from jax.experimental import pallas as pl
 from jax.experimental.pallas import tpu as pltpu
@@ -201,6 +202,631 @@
     )(*tables, *backs, latents, gate, out_w)
 
 
+MESH = pl.DeviceIdType.MESH
+ANY = pl.ANY
+
+FWD_ORDER = (2, 3, 1, 0)
+BWD_ORDER = (1, 0, 2, 3)
+
+
+def cas_values(length):
+    position = np.arange(length)
+    phase_angle = (position[:, None] * position[None, :] % length).astype(np.float32)
+    phase_angle = phase_angle * np.float32(2.0 * math.pi / length)
+    table = (np.cos(phase_angle) + np.sin(phase_angle)) / np.float32(math.sqrt(length))
+    return table.astype(jnp.bfloat16)
+
+
+def widened_values(table, copies):
+    return np.kron(table.astype(np.float32), np.eye(copies, dtype=np.float32)).astype(jnp.bfloat16)
+
+
+class Plan:
+    def __init__(self, n, rows, channels):
+        self.n = n
+        self.bits = n.bit_length() - 1
+        self.channels = channels
+        self.lines = rows // WW
+        self.band = WW // n
+        self.parts = 2
+        self.sub = self.band // self.parts
+        self.group = TILE // self.sub
+        self.groups = self.lines // self.group
+        self.block = self.lines * self.sub
+        self.frame = HH * self.sub
+        self.width = min(256, channels)
+        self.depth = channels // n
+
+
+def flow_kernel(
+    plan,
+    latents,
+    spectrum,
+    value_w,
+    gate_w,
+    out_w,
+    embed,
+    ids,
+    step_row,
+    bands,
+    bands_t,
+    height,
+    time,
+    sent,
+    planes,
+    filtered,
+    back,
+    out,
+    full,
+    full_rest,
+    pool_all,
+    lat,
+    embed_vm,
+    table,
+    table_t,
+    stage,
+    pv,
+    weight,
+    weight_out,
+    arrived,
+    residual,
+    result,
+    gains,
+    spec,
+    out_vm,
+    pool_vm,
+    pool_col,
+    scale,
+    lat_sem,
+    embed_sem,
+    own_sem,
+    stage_sem,
+    pv_sem,
+    gain_sem,
+    weight_sem,
+    out_sem,
+    misc_sem,
+    arrived_sem,
+    residual_sem,
+    result_sem,
+    ag_send,
+    ag_recv,
+    fwd_send,
+    fwd_recv,
+    bwd_send,
+    bwd_recv,
+):
+    n, channels, sub, block = plan.n, plan.channels, plan.sub, plan.block
+    lines, group, groups, width = plan.lines, plan.group, plan.groups, plan.width
+    me = lax.axis_index("sp")
+    local_copy = pltpu.make_async_copy
+
+    def remote(source, target, send, recv, peer):
+        return pltpu.make_async_remote_copy(
+            source, target, send, recv, device_id={"sp": peer}, device_id_type=MESH
+        )
+
+    quarter = n // 4
+    high, low = me // quarter, me % quarter
+
+    def far_high(turn):
+        swapped = high + 2 * (1 - 2 * (high // 2)) if turn >= 2 else high
+        return swapped + (1 - 2 * (swapped % 2)) if turn % 2 else swapped
+
+    def after(turn, j):
+        return far_high(turn) * quarter + (low + j) % quarter
+
+    def before(turn, j):
+        return far_high(turn) * quarter + (low + quarter - j) % quarter
+
+    def each_peer(body, order=(1, 0, 2, 3)):
+        for turn in order:
+
+            def one(j, carry, turn=turn):
+                body(turn, j)
+                return carry
+
+            lax.fori_loop(0 if turn else 1, quarter, one, 0)
+
+    barrier = pltpu.get_barrier_semaphore()
+
+    def greet(turn, j):
+        pl.semaphore_signal(
+            barrier, inc=1, device_id={"sp": after(turn, j)}, device_id_type=MESH
+        )
+
+    each_peer(greet)
+
+    owned = [
+        local_copy(value_w, full.at[me], own_sem.at[0]),
+        local_copy(gate_w, full_rest.at[me, 0], own_sem.at[1]),
+        local_copy(out_w, full_rest.at[me, 1], own_sem.at[2]),
+    ]
+    for copy in owned:
+        copy.start()
+    rows = group * WW
+
+    def lat_copy(g):
+        return local_copy(
+            latents.at[pl.ds(g * rows, rows), :], lat.at[pl.ds(g * rows, rows), :], lat_sem.at[g]
+        )
+
+    for g in range(groups):
+        lat_copy(g).start()
+    embed_in = local_copy(embed, embed_vm, embed_sem)
+    embed_in.start()
+
+    lanes = 128
+
+    def pool_part():
+        tokens = ids.shape[1]
+        highs = embed_vm.shape[1] // lanes
+        token = ids[...]
+        upper = lax.broadcasted_iota(jnp.int32, (highs, tokens), 0) == token // lanes
+        lower = lax.broadcasted_iota(jnp.int32, (lanes, tokens), 0) == token % lanes
+        counts = lax.dot_general(
+            upper.astype(jnp.float32).astype(jnp.bfloat16),
+            lower.astype(jnp.float32).astype(jnp.bfloat16),
+            (((1,), (1,)), ((), ())),
+            preferred_element_type=jnp.float32,
+        )
+        scale[...] = counts
+        embed_in.wait()
+
+        def pool_step(i, total):
+            first = pl.multiple_of(i * 8, 8)
+            some = scale[pl.ds(first, 8), :]
+            for k in range(8):
+                column = embed_vm[:, pl.ds(pl.multiple_of((first + k) * lanes, lanes), lanes)]
+                total += column.astype(jnp.float32) * some[k : k + 1, :]
+            return total
+
+        total = jnp.zeros((plan.depth, lanes), jnp.float32)
+        total = lax.fori_loop(0, highs // 8, pool_step, total)
+        pooled = jnp.sum(total, axis=1, keepdims=True) / tokens
+        pool_vm[...] = jnp.broadcast_to(pooled, (plan.depth, lanes))
+        pool_own = local_copy(pool_vm, pool_all.at[me], misc_sem)
+        pool_own.start()
+        pool_own.wait()
+
+    def doubling(i):
+        size = n >> (i + 1)
+        peer = me + size * (1 - 2 * ((me // size) % 2))
+        base = me % (2 * size)
+        return size, peer, base
+
+    gathered = (full, full_rest, pool_all)
+
+    def gather_start(k, i):
+        size, peer, base = doubling(i)
+        ref = gathered[k]
+
+        def one(j, carry):
+            owner = base + 2 * size * j
+            remote(ref.at[owner], ref.at[owner], ag_send.at[k, i], ag_recv.at[k, i], peer).start()
+            return carry
+
+        lax.fori_loop(0, 1 << i, one, 0)
+
+    def gather_wait(k, i):
+        _, peer, _ = doubling(i)
+        some = gathered[k].at[pl.ds(0, 1 << i)]
+        whole = remote(some, some, ag_send.at[k, i], ag_recv.at[k, i], peer)
+        whole.wait_send()
+        whole.wait_recv()
+
+    def build_tables(p):
+        wide, tall = n * group * sub, group * WW
+        row = lax.broadcasted_iota(jnp.int32, (wide, n * sub), 0)
+        column = lax.broadcasted_iota(jnp.int32, (wide, n * sub), 1)
+        pick = (row // (group * sub)) * sub + row % sub == column
+        pick = pick.astype(jnp.float32).astype(jnp.bfloat16)
+        spread = dot(pick, bands[p])
+        row = lax.broadcasted_iota(jnp.int32, (n * sub, wide), 0)
+        column = lax.broadcasted_iota(jnp.int32, (n * sub, wide), 1)
+        pick = (column // (group * sub)) * sub + column % sub == row
+        pick = pick.astype(jnp.float32).astype(jnp.bfloat16)
+        spread_t = dot(bands_t[p], pick)
+        line = lax.broadcasted_iota(jnp.int32, (wide, WW), 0) // sub % group
+        line_t = lax.broadcasted_iota(jnp.int32, (WW, wide), 1) // sub % group
+        for k in range(group):
+            table[:, k * WW : (k + 1) * WW] = jnp.where(line == k, spread, 0.0).astype(jnp.bfloat16)
+            table_t[p, k * WW : (k + 1) * WW, :] = jnp.where(line_t == k, spread_t, 0.0).astype(
+                jnp.bfloat16
+            )
+
+    def stage_copy(p, g):
+        slot = g % 2
+        some = pl.ds(pl.multiple_of(g * TILE, TILE), TILE)
+        return local_copy(stage.at[slot], sent.at[p, :, some, :], stage_sem.at[slot])
+
+    def fwd_copy(p, g, turn, j):
+        some = pl.ds(pl.multiple_of(g * TILE, TILE), TILE)
+        step = turn * quarter + j
+        return remote(
+            sent.at[p, after(turn, j), some, :],
+            planes.at[p, me, some, :],
+            fwd_send.at[p, g, step],
+            fwd_recv.at[p, g, step],
+            after(turn, j),
+        )
+
+    def width_group(p, g):
+        if p == 0:
+            lat_copy(g).wait()
+        moved = dot(table[...], lat[pl.ds(pl.multiple_of(g * rows, rows), rows), :])
+        stage[g % 2] = moved.reshape(n, TILE, channels).astype(jnp.bfloat16)
+        stage_copy(p, g).start()
+
+    def fwd_group(p, g):
+        stage_copy(p, g).wait()
+        each_peer(lambda turn, j: fwd_copy(p, g, turn, j).start(), FWD_ORDER)
+
+    def width_groups(p, first, last):
+        def one(g, carry):
+            width_group(p, g)
+
+            @pl.when(g > first)
+            def _():
+                fwd_group(p, g - 1)
+
+            return carry
+
+        lax.fori_loop(first, last, one, 0)
+
+    build_tables(0)
+    for copy in owned:
+        copy.wait()
+    pl.semaphore_wait(barrier, n - 1)
+    gather_start(0, 0)
+    gather_start(1, 0)
+    middle = max(1, groups // 2)
+    width_groups(0, 0, middle)
+    fwd_group(0, middle - 1)
+    gather_wait(0, 0)
+    gather_start(0, 1)
+    gather_wait(1, 0)
+    gather_start(1, 1)
+    width_groups(0, middle, groups)
+    fwd_group(0, groups - 1)
+    gather_wait(0, 1)
+    gather_start(0, 2)
+    build_tables(1)
+    width_groups(1, 0, groups)
+    fwd_group(1, groups - 1)
+    gather_wait(1, 1)
+    gather_start(1, 2)
+    pool_part()
+    gather_start(2, 0)
+    for i in range(2, plan.bits):
+        gather_wait(0, i)
+        if i + 1 < plan.bits:
+            gather_start(0, i + 1)
+    gather_wait(1, 2)
+    if plan.bits > 3:
+        gather_start(1, 3)
+    value_in = local_copy(full, weight.at[0], weight_sem.at[0])
+    value_in.start()
+    value_in.wait()
+
+    def gate_part():
+        rest_in = [
+            local_copy(full_rest.at[:, 0], weight.at[1], weight_sem.at[0]),
+            local_copy(full_rest.at[:, 1], weight_out, weight_sem.at[1]),
+            local_copy(pool_all, pool_col, misc_sem),
+        ]
+        for copy in rest_in:
+            copy.start()
+        for copy in rest_in:
+            copy.wait()
+        column = pool_col[...].reshape(channels, lanes)
+        scale_row = 1.0 + column.T[0:1, :] + step_row[...]
+        chunk = min(256, lines * WW)
+
+        def gate_step(i, carry):
+            some = pl.ds(pl.multiple_of(i * chunk, chunk), chunk)
+            value = dot(lat[some, :], weight[1].reshape(channels, channels))
+            value = value / (1.0 + jnp.exp(-value))
+            lat[some, :] = (value * scale_row).astype(jnp.bfloat16)
+            return carry
+
+        lax.fori_loop(0, lines * WW // chunk, gate_step, 0)
+
+    def gain_copy(cb):
+        slot = cb % 2
+        cols = pl.ds(pl.multiple_of(cb * width, width), width)
+        return local_copy(spectrum.at[:, :, :, cols], gains.at[slot], gain_sem.at[slot])
+
+    def bwd_copy(p, g, turn, j):
+        each = block if p + 1 < plan.parts else TILE
+        step = turn * quarter + j
+        start = pl.multiple_of(after(turn, j) * block + g * each, each)
+        target = back.at[p, me, pl.ds(pl.multiple_of(g * each, each), each), :]
+        return remote(
+            filtered.at[p, pl.ds(start, each), :],
+            target,
+            bwd_send.at[p, g, step],
+            bwd_recv.at[p, g, step],
+            after(turn, j),
+        )
+
+    blocks = channels // width
+    pieces = plan.frame // TILE
+
+    def plane_part(p):
+        def arrive(turn, j):
+            source = before(turn, j)
+
+            def one(g, carry):
+                fwd_copy(p, g, turn, j).wait_recv()
+                return carry
+
+            lax.fori_loop(0, groups, one, 0)
+            place = pl.ds(pl.multiple_of(source * block, block), block)
+            local_copy(planes.at[p, source], pv.at[place, :], pv_sem).start()
+
+        place = pl.ds(pl.multiple_of(me * block, block), block)
+        local_copy(sent.at[p, me], pv.at[place, :], pv_sem).start()
+        gain_copy(0).start()
+        each_peer(arrive)
+        local_copy(filtered.at[p], pv, pv_sem).wait()
+
+        def columns(cb, carry):
+            cols = pl.ds(pl.multiple_of(cb * width, width), width)
+            slot = cb % 2
+            gain_copy(cb).wait()
+
+            @pl.when(cb + 1 < blocks)
+            def _():
+                gain_copy(cb + 1).start()
+
+            def forward(t, inner):
+                some = pl.ds(pl.multiple_of(t * plan.frame, plan.frame), plan.frame)
+                w = weight[0, :, :, cols].reshape(channels, width)
+                value = dot(pv[some, :], w).astype(jnp.bfloat16)
+                spec[t] = dot(height[...], value).astype(jnp.bfloat16)
+                return inner
+
+            lax.fori_loop(0, TT, forward, 0, unroll=2)
+
+            def across(i, inner):
+                some = pl.ds(pl.multiple_of(i * TILE, TILE), TILE)
+                one = spec[:, some, :].reshape(TT * TILE, width)
+                whole = dot(time[...], one)
+                each = TILE // sub
+                gain = gains[
+                    slot,
+                    :,
+                    pl.ds(pl.multiple_of(i * each, each), each),
+                    p * sub : (p + 1) * sub,
+                    :,
+                ]
+                gain = gain.reshape(TT * TILE, width).astype(jnp.float32)
+                kept = (whole * gain).astype(jnp.bfloat16)
+                spec[:, some, :] = dot(time[...], kept).astype(jnp.bfloat16).reshape(TT, TILE, width)
+                return inner
+
+            lax.fori_loop(0, pieces, across, 0)
+
+            def backward(t, inner):
+                some = pl.ds(pl.multiple_of(t * plan.frame, plan.frame), plan.frame)
+                out_vm[some, cols] = dot(height[...], spec[t]).astype(jnp.bfloat16)
+                return inner
+
+            lax.fori_loop(0, TT, backward, 0, unroll=2)
+            return carry
+
+        lax.fori_loop(0, blocks, columns, 0)
+        own = local_copy(out_vm.at[place, :], back.at[p, me], own_sem.at[0])
+        whole = local_copy(out_vm, filtered.at[p], out_sem)
+        own.start()
+        whole.start()
+        whole.wait()
+        own.wait()
+
+        def send_group(g, carry):
+            each_peer(lambda turn, j: bwd_copy(p, g, turn, j).start(), BWD_ORDER)
+            return carry
+
+        lax.fori_loop(0, groups if p + 1 == plan.parts else 1, send_group, 0)
+
+    plane_part(0)
+    gather_wait(2, 0)
+    gather_start(2, 1)
+    for i in range(3, plan.bits):
+        gather_wait(1, i)
+        if i + 1 < plan.bits:
+            gather_start(1, i + 1)
+    plane_part(1)
+    gather_wait(2, 1)
+    gather_start(2, 2)
+    for i in range(2, plan.bits):
+        gather_wait(2, i)
+        if i + 1 < plan.bits:
+            gather_start(2, i + 1)
+    gate_part()
+
+    last = plan.parts - 1
+    each_peer(lambda turn, j: bwd_copy(0, 0, turn, j).wait_recv())
+
+    def residual_copy(g):
+        slot = g % 2
+        some = pl.ds(pl.multiple_of(g * rows, rows), rows)
+        return local_copy(latents.at[some, :], residual.at[slot], residual_sem.at[slot])
+
+    def result_copy(g):
+        slot = g % 2
+        some = pl.ds(pl.multiple_of(g * rows, rows), rows)
+        return local_copy(result.at[slot], out.at[some, :], result_sem.at[slot])
+
+    chunk = min(256, rows)
+    residual_copy(0).start()
+
+    def mix_group(g, carry):
+        slot = g % 2
+        each_peer(lambda turn, j: bwd_copy(last, g, turn, j).wait_recv())
+        some = pl.ds(pl.multiple_of(g * TILE, TILE), TILE)
+        inward = [
+            local_copy(back.at[p, :, some, :], arrived.at[p], arrived_sem.at[p])
+            for p in range(plan.parts)
+        ]
+        for copy in inward:
+            copy.start()
+
+        @pl.when(g + 1 < groups)
+        def _():
+            residual_copy(g + 1).start()
+
+        @pl.when(g >= 2)
+        def _():
+            result_copy(g - 2).wait()
+
+        residual_copy(g).wait()
+        for copy in inward:
+            copy.wait()
+
+        def mix_step(i, inner):
+            some = pl.ds(pl.multiple_of(i * chunk, chunk), chunk)
+            cells = pl.ds(pl.multiple_of(g * rows + i * chunk, chunk), chunk)
+            mix = 0.0
+            for p in range(plan.parts):
+                mix += dot(table_t[p, some, :], arrived[p].reshape(n * TILE, channels))
+            mixed = (mix * lat[cells, :].astype(jnp.float32)).astype(jnp.bfloat16)
+            projected = dot(mixed, weight_out[...].reshape(channels, channels))
+            total = residual[slot, some, :].astype(jnp.float32) + projected
+            result[slot, some, :] = total.astype(jnp.bfloat16)
+            return inner
+
+        lax.fori_loop(0, rows // chunk, mix_step, 0)
+        result_copy(g).start()
+        return carry
+
+    lax.fori_loop(0, groups, mix_group, 0)
+    for g in range(max(0, groups - 2), groups):
+        result_copy(g).wait()
+
+    for p in range(plan.parts):
+
+        def settle(g, carry, p=p):
+            each_peer(lambda turn, j: fwd_copy(p, g, turn, j).wait_send())
+            return carry
+
+        lax.fori_loop(0, groups, settle, 0)
+
+        def settle_back(g, carry, p=p):
+            each_peer(lambda turn, j: bwd_copy(p, g, turn, j).wait_send())
+            return carry
+
+        lax.fori_loop(0, groups if p == last else 1, settle_back, 0)
+
+
+def flow(plan, latents, spectrum, weights, embed, ids, step_row):
+    n, channels, parts = plan.n, plan.channels, plan.parts
+    wide, tall = n * plan.group * plan.sub, plan.group * WW
+    cells = latents.shape[0]
+    plane_rows = n * plan.block
+    bands = cas_values(WW).reshape(n, parts, plan.sub, WW).transpose(1, 0, 2, 3)
+    bands = bands.reshape(parts, n * plan.sub, WW)
+    bf, f32 = jnp.bfloat16, jnp.float32
+    vmem, dma = pltpu.VMEM, pltpu.SemaphoreType.DMA
+    whole = pl.BlockSpec(memory_space=vmem)
+    far = pl.BlockSpec(memory_space=ANY)
+    moving = (parts, n, plan.block, channels)
+    highs = embed.shape[1] // 128
+    outs = [
+        (moving, bf),
+        (moving, bf),
+        ((parts, plane_rows, channels), bf),
+        (moving, bf),
+        ((cells, channels), bf),
+        ((n, plan.depth, channels), bf),
+        ((n, 2, plan.depth, channels), bf),
+        ((n, plan.depth, 128), f32),
+    ]
+    return pl.pallas_call(
+        lambda *refs: flow_kernel(plan, *refs),
+        in_specs=[far, far, whole, whole, whole, far] + [whole] * 6,
+        out_specs=[far] * len(outs),
+        out_shape=[jax.ShapeDtypeStruct(shape, dtype) for shape, dtype in outs],
+        scratch_shapes=[
+            vmem((cells, channels), bf),
+            vmem(embed.shape, bf),
+            vmem((wide, tall), bf),
+            vmem((parts, tall, wide), bf),
+            vmem((2, n, TILE, channels), bf),
+            vmem((plane_rows, channels), bf),
+            vmem((2, n, plan.depth, channels), bf),
+            vmem((n, plan.depth, channels), bf),
+            vmem((parts, n, TILE, channels), bf),
+            vmem((2, tall, channels), bf),
+            vmem((2, tall, channels), bf),
+            vmem((2, TT, HH, plan.band, plan.width), bf),
+            vmem((TT, plan.frame, plan.width), bf),
+            vmem((plane_rows, channels), bf),
+            vmem((plan.depth, 128), f32),
+            vmem((n, plan.depth, 128), f32),
+            vmem((highs, 128), f32),
+            dma((plan.groups,)),
+            dma,
+            dma((3,)),
+            dma((2,)),
+            dma,
+            dma((2,)),
+            dma((2,)),
+            dma,
+            dma,
+            dma((parts,)),
+            dma((2,)),
+            dma((2,)),
+            dma((3, plan.bits)),
+            dma((3, plan.bits)),
+            dma((parts, plan.groups, n)),
+            dma((parts, plan.groups, n)),
+            dma((parts, plan.groups, n)),
+            dma((parts, plan.groups, n)),
+        ],
+        compiler_params=pltpu.CompilerParams(
+            collective_id=0, has_side_effects=True, vmem_limit_bytes=60 * 2**20
+        ),
+        name="flow",
+    )(
+        latents,
+        spectrum,
+        *weights,
+        embed,
+        ids,
+        step_row,
+        bands,
+        bands.transpose(0, 2, 1),
+        widened_values(cas_values(HH), plan.sub),
+        widened_values(cas_values(TT), TILE),
+    )
+
+
+def streamed(latents, spectrum, w_value, w_gate, w_out, embed_table, prompt_ids, noise_step):
+    rows, channels = latents.shape
+    plan = Plan(lax.axis_size("sp"), rows, channels)
+    channel = jnp.arange(channels, dtype=jnp.int32)
+    step_row = step_embedding(noise_step, channel, C)[None, :]
+    outs = flow(
+        plan,
+        latents,
+        spectrum,
+        (w_value, w_gate, w_out),
+        embed_table,
+        prompt_ids[None, :],
+        step_row,
+    )
+    return outs[4]
+
+
+def fits(mesh):
+    n = mesh.shape["sp"]
+    alone = mesh.shape["grp"] == 1 and mesh.shape["ch"] == 1
+    band = WW // n
+    return alone and n >= 8 and n & (n - 1) == 0 and band >= 2 and TT * HH // n * band >= 2 * TILE
+
+
 def exchange(blocks):
     return lax.all_to_all(blocks, "sp", split_axis=0, concat_axis=0, tiled=True)
 
@@ -310,5 +936,6 @@
         P("grp"),
     )
     return jax.shard_map(
-        local, mesh=mesh, in_specs=placed, out_specs=P(("grp", "sp", "ch"), None), check_vma=False
+        streamed if fits(mesh) else local,
+        mesh=mesh, in_specs=placed, out_specs=P(("grp", "sp", "ch"), None), check_vma=False
     )

time: 474 us -> 412 us (0.87)
  Pallas kernels: 127 us -> 398 us
  waiting for transfers between devices: 245 us -> 0 us
  local copies, waits for them, and re-layouts: 62.6 us -> 7.76 us
  starting transfers between devices: 19.8 us -> 0 us
  between operations: 14 us -> 0.66 us
    pallas_call x6 -> x1, Pallas kernels: 127 us -> 398 us  [flow(): pl.pallas_call(lambda *refs: flow_kernel(plan, *refs), in_specs=[far, far...]
    all_gather x3 -> x0, waiting for transfers between devices: 122 us -> none  [the longest x1 78.1 us: local(): full_value = lax.all_gather(w_value, 'sp', axis=0)]
    all_to_all x4 -> x0, waiting for transfers between devices: 122 us -> none  [exchange(): return lax.all_to_all(blocks, 'sp', split_axis=0, concat_axis=0, tiled=True)]
    all_to_all x4 -> x0, starting transfers between devices: 19.5 us -> none  [exchange(): return lax.all_to_all(blocks, 'sp', split_axis=0, concat_axis=0, tiled=True)]
    reshape x1 -> x0, local copies, waits for them, and re-layouts: 17.5 us -> none  [local(): gains = spectrum.reshape(TT, HH, parts, sub, chan_part)]
    another operation x2 -> x0, local copies, waits for them, and re-layouts: 14.4 us -> none  [local(): gains[:, :, part].reshape(TT, HH * sub, chan_part)]
    unnamed x16 -> x1, local copies, waits for them, and re-layouts: 18.4 us -> 7.76 us
    mul x7 -> x0, local copies, waits for them, and re-layouts: 7.1 us -> none  [the longest x2 5.4 us: widened(): both = table[:, None, :, None] * inner[None, :, None, :]]
  transfers between devices with their start and end apart: 7 -> 0, of which waited for: 7 -> 0; matrix products, arithmetic and copies ran while one was open for 13% -> 0% of each run, Pallas kernels for 21% -> 0%
where the time goes in v1:
time: 412 us; the launch traced here: 407 us
  Pallas kernels  398 us (97%)
  local copies, waits for them, and re-layouts  7.76 us (2%)
    pallas_call x1, Pallas kernels, flow(): pl.pallas_call(lambda *refs: flow_kernel(plan, *refs), in_specs=[far, far...  398 us

profile of v1, /device:TPU:0, one launch (start us, length us, event | category | flops | bytes accessed | tf_op | source)
XLA Modules:
  0.0 407.0 jit_solution(420272427812195419)
XLA Ops:
  0.7 0.7 compare_select_fusion.refs_7_
  1.4 397.8 %flow.1 = (bf16[2,32,64,1024]{3,2,1,0:T(8,128)(2,1)}, bf16[2,32,64,1024]{3,2,1,0:T(8,128)(2,1)}, bf16[2,2048,1024]{2,1,0:T(8,128)(2,1)}, bf16[2,32,64,1024]{3,2,...) custom-call(bf16[4096,1024]{1,0:T(8,128)(2,1)} %refs_0_.1, ...), custom_call_target="tpu_custom_call" | custom-call | tf_op jit(solution)/shard_map/flow/pallas_call | solution.py:746
  399.2 7.8 %copy.15 = bf16[4096,1024]{1,0:T(8,128)(2,1)} copy(bf16[4096,1024]{1,0:T(8,128)(2,1)} %get-tuple-element.6) | data formatting | bytes 16777216

commit v2 on v1

--- a/solution.py
+++ b/solution.py
@@ -205,8 +205,8 @@
 MESH = pl.DeviceIdType.MESH
 ANY = pl.ANY
 
-FWD_ORDER = (2, 3, 1, 0)
-BWD_ORDER = (1, 0, 2, 3)
+FWD_TURNS = (1, 2, 0, 3)
+BWD_TURNS = (1, 2, 0, 3)
 
 
 def cas_values(length):
@@ -246,12 +246,12 @@
     gate_w,
     out_w,
     embed,
-    ids,
-    step_row,
-    bands,
-    bands_t,
-    height,
-    time,
+    ids_far,
+    step_far,
+    bands_far,
+    bands_t_far,
+    height_far,
+    time_far,
     sent,
     planes,
     filtered,
@@ -260,7 +260,16 @@
     full,
     full_rest,
     pool_all,
+    tables_out,
+    gate_out,
     lat,
+    held,
+    ids,
+    step_row,
+    bands,
+    bands_t,
+    height,
+    time,
     embed_vm,
     table,
     table_t,
@@ -286,9 +295,13 @@
     weight_sem,
     out_sem,
     misc_sem,
+    small_sem,
+    tail_sem,
     arrived_sem,
     residual_sem,
     result_sem,
+    first_send,
+    first_recv,
     ag_send,
     ag_recv,
     fwd_send,
@@ -306,44 +319,66 @@
             source, target, send, recv, device_id={"sp": peer}, device_id_type=MESH
         )
 
+    flips = [(1 << b) * (1 - 2 * lax.rem(lax.div(me, 1 << b), 2)) for b in range(plan.bits)]
+
+    def paired(mask):
+        peer = me
+        for b in range(plan.bits):
+            peer += flips[b] * lax.rem(lax.div(mask, 1 << b), 2)
+        return peer
+
+    def each_mask(body):
+        def one(mask, carry):
+            body(mask)
+            return carry
+
+        lax.fori_loop(1, n, one, 0)
+
     quarter = n // 4
-    high, low = me // quarter, me % quarter
-
-    def far_high(turn):
-        swapped = high + 2 * (1 - 2 * (high // 2)) if turn >= 2 else high
-        return swapped + (1 - 2 * (swapped % 2)) if turn % 2 else swapped
-
-    def after(turn, j):
-        return far_high(turn) * quarter + (low + j) % quarter
-
-    def before(turn, j):
-        return far_high(turn) * quarter + (low + quarter - j) % quarter
-
-    def each_peer(body, order=(1, 0, 2, 3)):
-        for turn in order:
-
-            def one(j, carry, turn=turn):
-                body(turn, j)
-                return carry
-
-            lax.fori_loop(0 if turn else 1, quarter, one, 0)
+    chips = quarter // 2
+    core = lax.rem(me, 2)
+
+    def each_peer(body, turns):
+        def one(step, carry):
+            for i, turn in enumerate(turns):
+                chip = lax.rem(step + i, chips)
+                chip = chip + core * (chips - 1 - 2 * chip)
+                mask = turn * quarter + chip * 2 + lax.div(step, chips)
+
+                if turn:
+                    body(mask)
+                else:
+
+                    @pl.when(mask > 0)
+                    def _(mask=mask):
+                        body(mask)
+
+            return carry
+
+        lax.fori_loop(0, quarter, one, 0)
 
     barrier = pltpu.get_barrier_semaphore()
 
-    def greet(turn, j):
-        pl.semaphore_signal(
-            barrier, inc=1, device_id={"sp": after(turn, j)}, device_id_type=MESH
+    def greet(mask):
+        pl.semaphore_signal(barrier, inc=1, device_id={"sp": paired(mask)}, device_id_type=MESH)
+
+    each_mask(greet)
+
+    small = [
+        local_copy(source, target, small_sem.at[i])
+        for i, (source, target) in enumerate(
+            (
+                (bands_far, bands),
+                (bands_t_far, bands_t),
+                (ids_far, ids),
+                (height_far, height),
+                (time_far, time),
+                (step_far, step_row),
+            )
         )
-
-    each_peer(greet)
-
-    owned = [
-        local_copy(value_w, full.at[me], own_sem.at[0]),
-        local_copy(gate_w, full_rest.at[me, 0], own_sem.at[1]),
-        local_copy(out_w, full_rest.at[me, 1], own_sem.at[2]),
     ]
-    for copy in owned:
-        copy.start()
+    small[0].start()
+    small[1].start()
     rows = group * WW
 
     def lat_copy(g):
@@ -353,12 +388,21 @@
 
     for g in range(groups):
         lat_copy(g).start()
+    shards = (
+        (value_w, full.at[me]),
+        (gate_w, full_rest.at[me, 0]),
+        (out_w, full_rest.at[me, 1]),
+    )
+    shards_in = [local_copy(w, held.at[i], own_sem.at[i]) for i, (w, _) in enumerate(shards)]
+    owned = [local_copy(held.at[i], place, own_sem.at[i]) for i, (_, place) in enumerate(shards)]
     embed_in = local_copy(embed, embed_vm, embed_sem)
-    embed_in.start()
+    for copy in (*shards_in, *small[2:], embed_in):
+        copy.start()
 
     lanes = 128
 
     def pool_part():
+        small[2].wait()
         tokens = ids.shape[1]
         highs = embed_vm.shape[1] // lanes
         token = ids[...]
@@ -391,8 +435,8 @@
 
     def doubling(i):
         size = n >> (i + 1)
-        peer = me + size * (1 - 2 * ((me // size) % 2))
-        base = me % (2 * size)
+        peer = me + flips[plan.bits - 1 - i]
+        base = lax.rem(me, 2 * size)
         return size, peer, base
 
     gathered = (full, full_rest, pool_all)
@@ -407,6 +451,19 @@
             return carry
 
         lax.fori_loop(0, 1 << i, one, 0)
+
+    def gather_first():
+        _, peer, _ = doubling(0)
+        for i, (w, place) in enumerate(shards):
+            remote(w, place, first_send.at[i], first_recv.at[i], peer).start()
+
+    def gather_first_wait(i):
+        _, peer, _ = doubling(0)
+        w, place = shards[i]
+        copy = remote(w, place, first_send.at[i], first_recv.at[i], peer)
+        copy.wait_send()
+        copy.wait_recv()
+        owned[i].wait()
 
     def gather_wait(k, i):
         _, peer, _ = doubling(i)
@@ -440,15 +497,23 @@
         some = pl.ds(pl.multiple_of(g * TILE, TILE), TILE)
         return local_copy(stage.at[slot], sent.at[p, :, some, :], stage_sem.at[slot])
 
-    def fwd_copy(p, g, turn, j):
-        some = pl.ds(pl.multiple_of(g * TILE, TILE), TILE)
-        step = turn * quarter + j
+    last = plan.parts - 1
+    fwd_spans = [[(0, groups)] for _ in range(plan.parts)]
+    fwd_spans[0] = [(0, 1), (1, groups)]
+    bwd_spans = [[(0, groups)] for _ in range(plan.parts)]
+    cuts = list(range(groups + 1))
+    bwd_spans[last] = list(zip(cuts, cuts[1:]))
+
+    def fwd_copy(p, k, mask):
+        first, end = fwd_spans[p][k]
+        some = pl.ds(first * TILE, (end - first) * TILE)
+        peer = paired(mask)
         return remote(
-            sent.at[p, after(turn, j), some, :],
+            sent.at[p, peer, some, :],
             planes.at[p, me, some, :],
-            fwd_send.at[p, g, step],
-            fwd_recv.at[p, g, step],
-            after(turn, j),
+            fwd_send.at[p, k, mask],
+            fwd_recv.at[p, k, mask],
+            peer,
         )
 
     def width_group(p, g):
@@ -458,42 +523,43 @@
         stage[g % 2] = moved.reshape(n, TILE, channels).astype(jnp.bfloat16)
         stage_copy(p, g).start()
 
-    def fwd_group(p, g):
-        stage_copy(p, g).wait()
-        each_peer(lambda turn, j: fwd_copy(p, g, turn, j).start(), FWD_ORDER)
-
-    def width_groups(p, first, last):
+    def fwd_start(p, k):
+        each_peer(lambda mask: fwd_copy(p, k, mask).start(), FWD_TURNS)
+
+    def width_groups(p, first, end):
         def one(g, carry):
-            width_group(p, g)
-
             @pl.when(g > first)
             def _():
-                fwd_group(p, g - 1)
-
+                stage_copy(p, g - 1).wait()
+
+            width_group(p, g)
             return carry
 
-        lax.fori_loop(first, last, one, 0)
-
+        lax.fori_loop(first, end, one, 0)
+        stage_copy(p, end - 1).wait()
+
+    small[0].wait()
+    small[1].wait()
     build_tables(0)
-    for copy in owned:
-        copy.wait()
+    for i in range(3):
+        shards_in[i].wait()
+        owned[i].start()
     pl.semaphore_wait(barrier, n - 1)
-    gather_start(0, 0)
-    gather_start(1, 0)
-    middle = max(1, groups // 2)
-    width_groups(0, 0, middle)
-    fwd_group(0, middle - 1)
-    gather_wait(0, 0)
+    gather_first()
+    width_groups(0, 0, 1)
+    fwd_start(0, 0)
+    width_groups(0, 1, groups)
+    gather_first_wait(0)
     gather_start(0, 1)
-    gather_wait(1, 0)
+    gather_first_wait(1)
+    gather_first_wait(2)
     gather_start(1, 1)
-    width_groups(0, middle, groups)
-    fwd_group(0, groups - 1)
+    fwd_start(0, 1)
     gather_wait(0, 1)
     gather_start(0, 2)
     build_tables(1)
     width_groups(1, 0, groups)
-    fwd_group(1, groups - 1)
+    fwd_start(1, 0)
     gather_wait(1, 1)
     gather_start(1, 2)
     pool_part()
@@ -508,6 +574,8 @@
     value_in = local_copy(full, weight.at[0], weight_sem.at[0])
     value_in.start()
     value_in.wait()
+    small[3].wait()
+    small[4].wait()
 
     def gate_part():
         rest_in = [
@@ -519,6 +587,7 @@
             copy.start()
         for copy in rest_in:
             copy.wait()
+        small[5].wait()
         column = pool_col[...].reshape(channels, lanes)
         scale_row = 1.0 + column.T[0:1, :] + step_row[...]
         chunk = min(256, lines * WW)
@@ -537,38 +606,35 @@
         cols = pl.ds(pl.multiple_of(cb * width, width), width)
         return local_copy(spectrum.at[:, :, :, cols], gains.at[slot], gain_sem.at[slot])
 
-    def bwd_copy(p, g, turn, j):
-        each = block if p + 1 < plan.parts else TILE
-        step = turn * quarter + j
-        start = pl.multiple_of(after(turn, j) * block + g * each, each)
-        target = back.at[p, me, pl.ds(pl.multiple_of(g * each, each), each), :]
+    def bwd_copy(p, k, mask):
+        first, end = bwd_spans[p][k]
+        count = (end - first) * TILE
+        peer = paired(mask)
+        start = pl.multiple_of(peer * block + first * TILE, TILE)
         return remote(
-            filtered.at[p, pl.ds(start, each), :],
-            target,
-            bwd_send.at[p, g, step],
-            bwd_recv.at[p, g, step],
-            after(turn, j),
+            filtered.at[p, pl.ds(start, count), :],
+            back.at[p, me, pl.ds(first * TILE, count), :],
+            bwd_send.at[p, k, mask],
+            bwd_recv.at[p, k, mask],
+            peer,
         )
 
     blocks = channels // width
     pieces = plan.frame // TILE
 
     def plane_part(p):
-        def arrive(turn, j):
-            source = before(turn, j)
-
-            def one(g, carry):
-                fwd_copy(p, g, turn, j).wait_recv()
-                return carry
-
-            lax.fori_loop(0, groups, one, 0)
+        def arrive(mask):
+            source = paired(mask)
+
+            for k in range(len(fwd_spans[p])):
+                fwd_copy(p, k, mask).wait_recv()
             place = pl.ds(pl.multiple_of(source * block, block), block)
             local_copy(planes.at[p, source], pv.at[place, :], pv_sem).start()
 
         place = pl.ds(pl.multiple_of(me * block, block), block)
         local_copy(sent.at[p, me], pv.at[place, :], pv_sem).start()
         gain_copy(0).start()
-        each_peer(arrive)
+        each_mask(arrive)
         local_copy(filtered.at[p], pv, pv_sem).wait()
 
         def columns(cb, carry):
@@ -624,11 +690,8 @@
         whole.wait()
         own.wait()
 
-        def send_group(g, carry):
-            each_peer(lambda turn, j: bwd_copy(p, g, turn, j).start(), BWD_ORDER)
-            return carry
-
-        lax.fori_loop(0, groups if p + 1 == plan.parts else 1, send_group, 0)
+        for k in range(len(bwd_spans[p])):
+            each_peer(lambda mask, k=k: bwd_copy(p, k, mask).start(), BWD_TURNS)
 
     plane_part(0)
     gather_wait(2, 0)
@@ -646,8 +709,15 @@
             gather_start(2, i + 1)
     gate_part()
 
-    last = plan.parts - 1
-    each_peer(lambda turn, j: bwd_copy(0, 0, turn, j).wait_recv())
+    tail = [
+        local_copy(table_t, tables_out, tail_sem.at[0]),
+        local_copy(lat.at[pl.ds((groups - 1) * rows, rows), :], gate_out, tail_sem.at[1]),
+    ]
+    for copy in tail:
+        copy.start()
+
+    for p in range(last):
+        each_mask(lambda mask, p=p: bwd_copy(p, 0, mask).wait_recv())
 
     def residual_copy(g):
         slot = g % 2
@@ -664,7 +734,6 @@
 
     def mix_group(g, carry):
         slot = g % 2
-        each_peer(lambda turn, j: bwd_copy(last, g, turn, j).wait_recv())
         some = pl.ds(pl.multiple_of(g * TILE, TILE), TILE)
         inward = [
             local_copy(back.at[p, :, some, :], arrived.at[p], arrived_sem.at[p])
@@ -673,7 +742,7 @@
         for copy in inward:
             copy.start()
 
-        @pl.when(g + 1 < groups)
+        @pl.when(g + 2 < groups)
         def _():
             residual_copy(g + 1).start()
 
@@ -701,23 +770,20 @@
         result_copy(g).start()
         return carry
 
-    lax.fori_loop(0, groups, mix_group, 0)
-    for g in range(max(0, groups - 2), groups):
+    for k, (first, end) in enumerate(bwd_spans[last][:-1]):
+        each_mask(lambda mask, k=k: bwd_copy(last, k, mask).wait_recv())
+        lax.fori_loop(first, end, mix_group, 0)
+    for g in range(max(0, groups - 3), groups - 1):
         result_copy(g).wait()
+    for copy in tail:
+        copy.wait()
 
     for p in range(plan.parts):
-
-        def settle(g, carry, p=p):
-            each_peer(lambda turn, j: fwd_copy(p, g, turn, j).wait_send())
-            return carry
-
-        lax.fori_loop(0, groups, settle, 0)
-
-        def settle_back(g, carry, p=p):
-            each_peer(lambda turn, j: bwd_copy(p, g, turn, j).wait_send())
-            return carry
-
-        lax.fori_loop(0, groups if p == last else 1, settle_back, 0)
+        for k in range(len(fwd_spans[p])):
+            each_mask(lambda mask, p=p, k=k: fwd_copy(p, k, mask).wait_send())
+        for k in range(len(bwd_spans[p])):
+            each_mask(lambda mask, p=p, k=k: bwd_copy(p, k, mask).wait_send())
+    each_mask(lambda mask: bwd_copy(last, len(bwd_spans[last]) - 1, mask).wait_recv())
 
 
 def flow(plan, latents, spectrum, weights, embed, ids, step_row):
@@ -729,7 +795,6 @@
     bands = bands.reshape(parts, n * plan.sub, WW)
     bf, f32 = jnp.bfloat16, jnp.float32
     vmem, dma = pltpu.VMEM, pltpu.SemaphoreType.DMA
-    whole = pl.BlockSpec(memory_space=vmem)
     far = pl.BlockSpec(memory_space=ANY)
     moving = (parts, n, plan.block, channels)
     highs = embed.shape[1] // 128
@@ -738,18 +803,27 @@
         (moving, bf),
         ((parts, plane_rows, channels), bf),
         (moving, bf),
-        ((cells, channels), bf),
+        ((cells - tall, channels), bf),
         ((n, plan.depth, channels), bf),
         ((n, 2, plan.depth, channels), bf),
         ((n, plan.depth, 128), f32),
+        ((parts, tall, wide), bf),
+        ((tall, channels), bf),
     ]
     return pl.pallas_call(
         lambda *refs: flow_kernel(plan, *refs),
-        in_specs=[far, far, whole, whole, whole, far] + [whole] * 6,
+        in_specs=[far] * 12,
         out_specs=[far] * len(outs),
         out_shape=[jax.ShapeDtypeStruct(shape, dtype) for shape, dtype in outs],
         scratch_shapes=[
             vmem((cells, channels), bf),
+            vmem((3, plan.depth, channels), bf),
+            vmem(ids.shape, jnp.int32),
+            vmem(step_row.shape, f32),
+            vmem(bands.shape, bf),
+            vmem((parts, WW, n * plan.sub), bf),
+            vmem((plan.frame, plan.frame), bf),
+            vmem((TT * TILE, TT * TILE), bf),
             vmem(embed.shape, bf),
             vmem((wide, tall), bf),
             vmem((parts, tall, wide), bf),
@@ -775,13 +849,17 @@
             dma((2,)),
             dma,
             dma,
+            dma((6,)),
+            dma((2,)),
             dma((parts,)),
             dma((2,)),
             dma((2,)),
+            dma((3,)),
+            dma((3,)),
             dma((3, plan.bits)),
             dma((3, plan.bits)),
-            dma((parts, plan.groups, n)),
-            dma((parts, plan.groups, n)),
+            dma((parts, 2, n)),
+            dma((parts, 2, n)),
             dma((parts, plan.groups, n)),
             dma((parts, plan.groups, n)),
         ],
@@ -803,6 +881,128 @@
     )
 
 
+def finish_kernel(
+    plan,
+    done,
+    back,
+    tables,
+    gate,
+    rest,
+    latents,
+    out,
+    arrived,
+    table,
+    scale,
+    weight,
+    residual,
+    result,
+    held,
+    back_sem,
+    table_sem,
+    scale_sem,
+    weight_sem,
+    residual_sem,
+    result_sem,
+    held_in,
+    held_out,
+):
+    n, channels, parts = plan.n, plan.channels, plan.parts
+    rows = plan.group * WW
+    first = (plan.groups - 1) * rows
+    chunk = min(256, rows)
+    copy = pltpu.make_async_copy
+    count = rows // chunk
+    inward = [
+        copy(back.at[p, :, pl.ds((plan.groups - 1) * TILE, TILE), :], arrived.at[p], back_sem.at[p])
+        for p in range(parts)
+    ]
+    weight_in = copy(rest.at[:, 1], weight, weight_sem)
+    steps = []
+    for i in range(count):
+        some = pl.ds(i * chunk, chunk)
+        steps.append(
+            [
+                copy(tables.at[:, some, :], table.at[:, some, :], table_sem.at[i]),
+                copy(gate.at[some, :], scale.at[some, :], scale_sem.at[i]),
+                copy(
+                    latents.at[pl.ds(first + i * chunk, chunk), :],
+                    residual.at[some, :],
+                    residual_sem.at[i],
+                ),
+            ]
+        )
+    passing = range(plan.groups - 1)
+    into = [copy(done.at[pl.ds(k * rows, rows), :], held.at[k], held_in.at[k]) for k in passing]
+    onward = [copy(held.at[k], out.at[pl.ds(k * rows, rows), :], held_out.at[k]) for k in passing]
+    for one in (*inward, steps[0][0], weight_in, *steps[0][1:]):
+        one.start()
+    for step in steps[1:]:
+        for one in step:
+            one.start()
+    for one in into:
+        one.start()
+    for one in inward:
+        one.wait()
+    results = []
+    for i in range(count):
+        some = pl.ds(i * chunk, chunk)
+        for one in steps[i]:
+            one.wait()
+        mix = 0.0
+        for p in range(parts):
+            mix += dot(table[p, some, :], arrived[p].reshape(n * TILE, channels))
+        mixed = (mix * scale[some, :].astype(jnp.float32)).astype(jnp.bfloat16)
+        if i == 0:
+            weight_in.wait()
+        projected = dot(mixed, weight[...].reshape(channels, channels))
+        total = residual[some, :].astype(jnp.float32) + projected
+        result[some, :] = total.astype(jnp.bfloat16)
+        results.append(
+            copy(
+                result.at[some, :], out.at[pl.ds(first + i * chunk, chunk), :], result_sem.at[i]
+            )
+        )
+        results[-1].start()
+        for k in passing:
+            if k % count == i:
+                into[k].wait()
+                onward[k].start()
+    for one in (*results, *onward):
+        one.wait()
+
+
+def finish(plan, done, back, tables, gate, rest, latents):
+    n, channels, parts = plan.n, plan.channels, plan.parts
+    rows = plan.group * WW
+    count = rows // min(256, rows)
+    bf, vmem, dma = jnp.bfloat16, pltpu.VMEM, pltpu.SemaphoreType.DMA
+    return pl.pallas_call(
+        lambda *refs: finish_kernel(plan, *refs),
+        in_specs=[pl.BlockSpec(memory_space=ANY)] * 6,
+        out_specs=pl.BlockSpec(memory_space=ANY),
+        out_shape=jax.ShapeDtypeStruct(latents.shape, bf),
+        scratch_shapes=[
+            vmem((parts, n, TILE, channels), bf),
+            vmem(tables.shape, bf),
+            vmem((rows, channels), bf),
+            vmem((n, plan.depth, channels), bf),
+            vmem((rows, channels), bf),
+            vmem((rows, channels), bf),
+            vmem((plan.groups - 1, rows, channels), bf),
+            dma((parts,)),
+            dma((count,)),
+            dma((count,)),
+            dma,
+            dma((count,)),
+            dma((count,)),
+            dma((plan.groups - 1,)),
+            dma((plan.groups - 1,)),
+        ],
+        compiler_params=pltpu.CompilerParams(vmem_limit_bytes=60 * 2**20),
+        name="finish",
+    )(done, back, tables, gate, rest, latents)
+
+
 def streamed(latents, spectrum, w_value, w_gate, w_out, embed_table, prompt_ids, noise_step):
     rows, channels = latents.shape
     plan = Plan(lax.axis_size("sp"), rows, channels)
@@ -817,14 +1017,15 @@
         prompt_ids[None, :],
         step_row,
     )
-    return outs[4]
+    _, _, _, back, done, _, rest, _, tables, gate = outs
+    return finish(plan, done, back, tables, gate, rest, latents)
 
 
 def fits(mesh):
     n = mesh.shape["sp"]
     alone = mesh.shape["grp"] == 1 and mesh.shape["ch"] == 1
     band = WW // n
-    return alone and n >= 8 and n & (n - 1) == 0 and band >= 2 and TT * HH // n * band >= 2 * TILE
+    return alone and n >= 8 and n & (n - 1) == 0 and band >= 2 and TT * HH // n * band >= 4 * TILE
 
 
 def exchange(blocks):

time: 412 us -> 398 us (0.966); the launches traced: 407 us -> 398 us
  local copies, waits for them, and re-layouts: 7.76 us -> 0 us
    unnamed x1 -> x0, local copies, waits for them, and re-layouts: 7.76 us -> none
    pallas_call x1 -> x2, Pallas kernels: 398 us -> 396 us  [the longest x1 386 us: flow(): pl.pallas_call(lambda *refs: flow_kernel(plan, *refs), in_specs=[far] * 1...]
where the time goes in v2:
time: 398 us
  Pallas kernels  396 us (99%)
    pallas_call x1, Pallas kernels, flow(): pl.pallas_call(lambda *refs: flow_kernel(plan, *refs), in_specs=[far] * 1...  386 us
    pallas_call x1, Pallas kernels, finish(): pl.pallas_call(lambda *refs: finish_kernel(plan, *refs), in_specs=[pl.Blo...  10.4 us

profile of v2, /device:TPU:0, one launch (start us, length us, event | category | flops | bytes accessed | tf_op | source)
XLA Modules:
  0.0 397.6 jit_solution(16216866346886114177)
XLA Ops:
  0.7 0.7 compare_select_fusion.refs_7_
  1.4 385.6 %flow.1 = (bf16[2,32,64,1024]{3,2,1,0:T(8,128)(2,1)}, bf16[2,32,64,1024]{3,2,1,0:T(8,128)(2,1)}, bf16[2,2048,1024]{2,1,0:T(8,128)(2,1)}, bf16[2,32,64,1024]{3,2,...) custom-call(bf16[4096,1024]{1,0:T(8,128)(2,1)} %refs_5_.3, ...), custom_call_target="tpu_custom_call" | custom-call | tf_op jit(solution)/shard_map/flow/pallas_call | solution.py:813
  387.0 10.4 %finish.1 = bf16[4096,1024]{1,0:T(8,128)(2,1)} custom-call(bf16[3072,1024]{1,0:T(8,128)(2,1)} %get-tuple-element.10.refs_0_, bf16[2,32,64,1024]{3,2,1,0:T(8,128)(2,1)} %get-tuple-element.11.refs_1_, bf16[2,1024,512]{2,1,0:T(8,128)(2,1)} %get-tuple-element.12.refs_2_, bf16[1024,1024]{1,0:T(8,128)(2,1)} %get-tuple-element.13.refs_3_, ...), custom_call_target="tpu_custom_call" | custom-call | tf_op jit(solution)/shard_map/finish/pallas_call | solution.py:979
